TPU v7x, 32 devices: a whole 2x2x4 slice. The times are simulated.
32 devices in a mesh: row: 4 (over x, core), col: 8 (over z, y).
Axes of the slice: x: 2, y: 2, z: 4, core: 2. Of those that a mesh axis runs over, the one named last changes fastest.
Arguments:
- inputs: bfloat16 [512, 8192], P('col', 'row'), may hold values from -6 to 6
- cotangent: bfloat16 [512, 8192], P('col', 'row'), may hold values from -6 to 6
- gate_pre: bfloat16 [512, 16384], P('row', 'col'), may hold values from -8 to 8
- up_pre: bfloat16 [512, 16384], P('row', 'col'), may hold values from -6 to 6
- w_gate: bfloat16 [8192, 16384], P('row', 'col'), may hold values from -0.0625 to 0.0625
- w_up: bfloat16 [8192, 16384], P('row', 'col'), may hold values from -0.0625 to 0.0625
- w_down: bfloat16 [16384, 8192], P('col', 'row'), may hold values from -0.046875 to 0.046875
Outputs:
- grad_inputs: bfloat16 [512, 8192], P('col', 'row')
- grad_gate: float32 [8192, 16384], P('row', 'col')
- grad_up: float32 [8192, 16384], P('row', 'col')
- grad_down: float32 [16384, 8192], P('col', 'row')
All inputs are finite; a program needn't handle non-finite values.
Results may differ from a plain program's by a relative error of at most 0.0049.
Values may be sent and summed in bfloat16 or wider, within the bound.
A program may use at most 128 MiB of HBM per device.

v0:
```python
import math
import jax
import jax.numpy as jnp
from jax import lax
from jax.sharding import PartitionSpec as P


def swiglu_back(gate_pre, up_pre, grad_hidden):
    gate_f = gate_pre.astype(jnp.float32)
    up_f = up_pre.astype(jnp.float32)
    sig = jax.nn.sigmoid(gate_f)
    act = gate_f * sig
    hidden = (act * up_f).astype(jnp.bfloat16)
    grad_gate_pre = (grad_hidden * up_f * sig * (1.0 + gate_f * (1.0 - sig))).astype(jnp.bfloat16)
    grad_up_pre = (grad_hidden * act).astype(jnp.bfloat16)
    return (hidden, grad_gate_pre, grad_up_pre)


def contract_last(left, right):
    return lax.dot_general(
        left, right, (((1,), (1,)), ((), ())), preferred_element_type=jnp.float32
    )


def contract_first(left, right):
    return lax.dot_general(
        left, right, (((0,), (0,)), ((), ())), preferred_element_type=jnp.float32
    )


def per_device(inputs, cotangent, gate_pre, up_pre, w_gate, w_up, w_down):
    inputs_all, cotan_all = (
        lax.all_gather(inputs, "col", axis=0, tiled=True),
        lax.all_gather(cotangent, "col", axis=0, tiled=True),
    )
    grad_hidden = lax.psum_scatter(
        contract_last(cotan_all, w_down), "row", scatter_dimension=0, tiled=True
    )
    hidden, grad_gate_pre, grad_up_pre = swiglu_back(gate_pre, up_pre, grad_hidden)
    hidden_all, gate_grad_all, up_grad_all = (
        lax.all_gather(hidden, "row", axis=0, tiled=True),
        lax.all_gather(grad_gate_pre, "row", axis=0, tiled=True),
        lax.all_gather(grad_up_pre, "row", axis=0, tiled=True),
    )
    grad_inputs = lax.psum_scatter(
        contract_last(gate_grad_all, w_gate) + contract_last(up_grad_all, w_up),
        "col",
        scatter_dimension=0,
        tiled=True,
    )
    scale = 1.0 / math.sqrt(inputs_all.shape[0])
    grad_gate = contract_first(inputs_all, gate_grad_all) * scale
    grad_up = contract_first(inputs_all, up_grad_all) * scale
    grad_down = contract_first(hidden_all, cotan_all) * scale
    return (grad_inputs.astype(jnp.bfloat16), grad_gate, grad_up, grad_down)


def solution(mesh):
    in_specs = (
        P("col", "row"),
        P("col", "row"),
        P("row", "col"),
        P("row", "col"),
        P("row", "col"),
        P("row", "col"),
        P("col", "row"),
    )
    out_specs = (P("col", "row"), P("row", "col"), P("row", "col"), P("col", "row"))
    return jax.shard_map(
        per_device, mesh=mesh, in_specs=in_specs, out_specs=out_specs, check_vma=False
    )
```

profile of v0, /device:TPU:0, one launch (start us, length us, event | category | flops | bytes accessed | tf_op | source)
XLA Modules:
  0.0 340.3 jit_solution(5187956274251306020)
XLA Ops:
  7.2 0.0 all-gather.6.cloned.1.call-start
  7.2 0.7 all-gather.6.cloned.1.call-update
  7.9 0.0 reduce-scatter.3.cloned.1.call-start
  7.9 54.0 %all-gather.6.cloned.1.call-done = bf16[512,2048]{1,0:T(8,128)(2,1)} async-done(((bf16[64,2048]{1,0:T(8,128)(2,1)}), bf16[512,2048]{1,0:T(8,128)(2,1)}) %all-gather.6.cloned.1.call-update) | async-done | bytes 2097168 | tf_op jit(solution)/shard_map/all_gather | solution.py:34
  61.9 10.6 %fusion.8 = f32[512,2048]{1,0:T(8,128)} fusion(bf16[512,2048]{1,0:T(8,128)(2,1)} %all-gather.6.cloned.1.call-done, bf16[2048,2048]{1,0:T(8,128)(2,1)} %param.13), kind=kOutput, calls=%fused_computation.18 | convolution fusion | flops 4294967296 | bytes 14680064 | tf_op jit(solution)/shard_map/dot_general | solution.py:20
  72.5 0.0 reduce-scatter.3.cloned.1.call-update
  72.5 0.0 all-gather.8.cloned.1.call-start
  72.6 43.2 %reduce-scatter.3.cloned.1.call-done = f32[128,2048]{1,0:T(8,128)} async-done(((f32[512,2048]{1,0:T(8,128)}), f32[128,2048]{1,0:T(8,128)}) %reduce-scatter.3.cloned.1.call-update) | async-done | bytes 1048592 | tf_op jit(solution)/shard_map/reduce_scatter | solution.py:36
  115.8 0.0 copy-done
  115.8 2.9 multiply_convert_fusion
  118.7 0.0 all-gather.8.cloned.1.call-update
  118.8 0.0 all-gather.10.cloned.1.call-start
  118.8 0.5 all-gather.10.cloned.1.call-update
  119.3 0.0 all-gather.12.cloned.1.call-start
  119.4 0.5 all-gather.12.cloned.1.call-update
  119.9 0.0 all-gather.14.cloned.1.call-start
  120.0 0.5 all-gather.14.cloned.1.call-update
  120.5 0.2 reduce-scatter.5.cloned.1.call-start
  120.7 20.7 %all-gather.8.cloned.1.call-done = bf16[512,2048]{1,0:T(8,128)(2,1)} async-done(((bf16[128,2048]{1,0:T(8,128)(2,1)}), bf16[512,2048]{1,0:T(8,128)(2,1)}) %all-gather.8.cloned.1.call-update) | async-done | bytes 2097168 | tf_op jit(solution)/shard_map/all_gather | solution.py:42
  141.5 10.6 %fusion.9 = f32[512,2048]{1,0:T(8,128)} fusion(bf16[512,2048]{1,0:T(8,128)(2,1)} %all-gather.8.cloned.1.call-done, bf16[2048,2048]{1,0:T(8,128)(2,1)} %param.11), kind=kOutput, calls=%fused_computation.19 | convolution fusion | flops 4294967296 | bytes 14680064 | tf_op jit(solution)/shard_map/dot_general | solution.py:20
  152.0 14.0 %all-gather.10.cloned.1.call-done = bf16[512,2048]{1,0:T(8,128)(2,1)} async-done(((bf16[128,2048]{1,0:T(8,128)(2,1)}), bf16[512,2048]{1,0:T(8,128)(2,1)}) %all-gather.10.cloned.1.call-update) | async-done | bytes 2097168 | tf_op jit(solution)/shard_map/all_gather | solution.py:43
  166.1 11.6 %convolution_add_fusion = f32[512,2048]{1,0:T(8,128)} fusion(f32[512,2048]{1,0:T(8,128)} %fusion.9, bf16[512,2048]{1,0:T(8,128)(2,1)} %all-gather.10.cloned.1.call-done, bf16[2048,2048]{1,0:T(8,128)(2,1)} %param.12), kind=kOutput, calls=%fused_computation.3 | convolution fusion | flops 4296015872 | bytes 18874368 | tf_op jit(solution)/shard_map/dot_general | solution.py:20
  177.7 0.0 reduce-scatter.5.cloned.1.call-update
  177.7 39.4 %all-gather.12.cloned.1.call-done = bf16[512,2048]{1,0:T(8,128)(2,1)} async-done(((bf16[64,2048]{1,0:T(8,128)(2,1)}), bf16[512,2048]{1,0:T(8,128)(2,1)}) %all-gather.12.cloned.1.call-update) | async-done | bytes 2097168 | tf_op jit(solution)/shard_map/all_gather | solution.py:33
  217.2 10.1 %multiply_bitcast_fusion.1 = f32[2048,2048]{0,1:T(8,128)} fusion(bf16[512,2048]{1,0:T(8,128)(2,1)S(1)} %copy-done.3, bf16[512,2048]{1,0:T(8,128)(2,1)} %all-gather.12.cloned.1.call-done), kind=kOutput, calls=%fused_computation.1 | convolution fusion | flops 4299161600 | bytes 20971520 | tf_op jit(solution)/shard_map/dot_general | solution.py:26
  227.3 17.8 %copy.11 = f32[2048,2048]{1,0:T(8,128)} copy(f32[2048,2048]{0,1:T(8,128)} %multiply_bitcast_fusion.1) | data formatting | bytes 33554432
  245.1 0.0 copy-done.4
  245.1 10.1 %multiply_bitcast_fusion = f32[2048,2048]{0,1:T(8,128)} fusion(bf16[512,2048]{1,0:T(8,128)(2,1)S(1)} %copy-done.4, bf16[512,2048]{1,0:T(8,128)(2,1)} %all-gather.12.cloned.1.call-done), kind=kOutput, calls=%fused_computation | convolution fusion | flops 4299161600 | bytes 20971520 | tf_op jit(solution)/shard_map/dot_general | solution.py:26
  255.2 17.9 %copy.12 = f32[2048,2048]{1,0:T(8,128)} copy(f32[2048,2048]{0,1:T(8,128)} %multiply_bitcast_fusion) | data formatting | bytes 33554432
  273.1 10.2 %convolution_multiply_fusion = f32[2048,2048]{1,0:T(8,128)} fusion(bf16[512,2048]{1,0:T(8,128)(2,1)} %all-gather.14.cloned.1.call-done, bf16[512,2048]{1,0:T(8,128)(2,1)S(1)} %copy-done.2), kind=kOutput, calls=%fused_computation.2 | convolution fusion | flops 4299161600 | bytes 20971520 | tf_op jit(solution)/shard_map/dot_general | solution.py:26
  283.2 48.4 %reduce-scatter.5.cloned.1.call-done = f32[64,2048]{1,0:T(8,128)} async-done(((f32[512,2048]{1,0:T(8,128)}), f32[64,2048]{1,0:T(8,128)}) %reduce-scatter.5.cloned.1.call-update) | async-done | bytes 524304 | tf_op jit(solution)/shard_map/reduce_scatter | solution.py:45
  331.7 1.8 convert_element_type.22
  (9 shorter events, 0.0 us)
Async XLA Ops:
  7.2 54.8 %all-gather.6.cloned.1.call-start = ((), (), s32[]{:S(2)}) async-start(), calls=%async_computation.2 | async-start | bytes 2359296 | tf_op jit(solution)/shard_map/all_gather | solution.py:34
  7.9 107.9 %reduce-scatter.3.cloned.1.call-start = ((), (), s32[]{:S(2)}) async-start(), calls=%async_computation.3 | async-start | bytes 5242880 | tf_op jit(solution)/shard_map/reduce_scatter | solution.py:36
  72.5 43.3 %copy-start = (bf16[128,2048]{1,0:T(8,128)(2,1)S(1)}, bf16[128,2048]{1,0:T(8,128)(2,1)}, u32[]{:S(2)}) copy-start(bf16[128,2048]{1,0:T(8,128)(2,1)} %param.9) | copy-start | bytes 1572868
  72.5 43.3 %copy-start.1 = (bf16[128,2048]{1,0:T(8,128)(2,1)S(1)}, bf16[128,2048]{1,0:T(8,128)(2,1)}, u32[]{:S(2)}) copy-start(bf16[128,2048]{1,0:T(8,128)(2,1)} %param.10) | copy-start | bytes 1572868
  72.5 68.9 %all-gather.8.cloned.1.call-start = ((), (), s32[]{:S(2)}) async-start(), calls=%async_computation.4 | async-start | bytes 2621440 | tf_op jit(solution)/shard_map/all_gather | solution.py:42
  118.8 47.3 %all-gather.10.cloned.1.call-start = ((), (), s32[]{:S(2)}) async-start(), calls=%async_computation.5 | async-start | bytes 2621440 | tf_op jit(solution)/shard_map/all_gather | solution.py:43
  119.3 97.8 %all-gather.12.cloned.1.call-start = ((), (), s32[]{:S(2)}) async-start(), calls=%async_computation.7 | async-start | bytes 2359296 | tf_op jit(solution)/shard_map/all_gather | solution.py:33
  119.9 153.2 %all-gather.14.cloned.1.call-start = ((), (), s32[]{:S(2)}) async-start(), calls=%async_computation.8 | async-start | bytes 2621440 | tf_op jit(solution)/shard_map/all_gather | solution.py:41
  120.5 211.2 %reduce-scatter.5.cloned.1.call-start = ((), (), s32[]{:S(2)}) async-start(), calls=%async_computation.6 | async-start | bytes 4718592 | tf_op jit(solution)/shard_map/reduce_scatter | solution.py:45
  177.7 39.5 %copy-start.3 = (bf16[512,2048]{1,0:T(8,128)(2,1)S(1)}, bf16[512,2048]{1,0:T(8,128)(2,1)}, u32[]{:S(2)}) copy-start(bf16[512,2048]{1,0:T(8,128)(2,1)} %all-gather.8.cloned.1.call-done) | copy-start | bytes 6291460
  227.3 17.8 %copy-start.4 = (bf16[512,2048]{1,0:T(8,128)(2,1)S(1)}, bf16[512,2048]{1,0:T(8,128)(2,1)}, u32[]{:S(2)}) copy-start(bf16[512,2048]{1,0:T(8,128)(2,1)} %all-gather.10.cloned.1.call-done) | copy-start | bytes 6291460
  255.2 17.9 %copy-start.2 = (bf16[512,2048]{1,0:T(8,128)(2,1)S(1)}, bf16[512,2048]{1,0:T(8,128)(2,1)}, u32[]{:S(2)}) copy-start(bf16[512,2048]{1,0:T(8,128)(2,1)} %all-gather.6.cloned.1.call-done) | copy-start | bytes 6291460
Sparse Core Ops, SparseCore 0:
  10.1 51.7 all-gather.5
  72.7 43.1 reduce-scatter.2
  118.9 22.5 all-gather.7
  143.5 22.5 all-gather.9
  168.0 49.0 all-gather.11
  218.6 21.0 all-gather.13
  243.3 88.2 reduce-scatter.4
where the time goes:
time: 341 us; the launch traced here: 340 us
  waiting for transfers between devices  222 us (65%)
  matrix products  63.2 us (19%)
  local copies, waits for them, and re-layouts  35.6 us (10%)
  between operations  14.1 us (4%)
  other arithmetic  4.69 us (1%)
    all_gather x1, waiting for transfers between devices, per_device(): lax.all_gather(cotangent, 'col', axis=0, tiled=True)  54 us
    reduce_scatter x1, waiting for transfers between devices, per_device(): lax.psum_scatter(contract_last(gate_grad_all, w_gate) + contract_last(up_...  48.4 us
    reduce_scatter x1, waiting for transfers between devices, per_device(): lax.psum_scatter(contract_last(cotan_all, w_down), 'row', scatter_dimensi...  43.2 us
    all_gather x1, waiting for transfers between devices, per_device(): lax.all_gather(inputs, 'col', axis=0, tiled=True)  39.4 us
    unnamed x12, local copies, waits for them, and re-layouts  35.6 us
    dot_general x3, matrix products, contract_last(): lax.dot_general(left, right, (((1,), (1,)), ((), ())), preferred_element_...  32.8 us
    dot_general x3, matrix products, contract_first(): lax.dot_general(left, right, (((0,), (0,)), ((), ())), preferred_element_...  30.4 us
    all_gather x1, waiting for transfers between devices, per_device(): lax.all_gather(grad_gate_pre, 'row', axis=0, tiled=True)  20.7 us
  transfers between devices with their start and end apart: 7, of which 6 were waited for; matrix products, arithmetic and copies ran while one was open for 26% of the time, Pallas kernels for 0%

commit v1 on v0

--- a/solution.py
+++ b/solution.py
@@ -30,7 +30,9 @@
 
 def per_device(inputs, cotangent, gate_pre, up_pre, w_gate, w_up, w_down):
     inputs_all, cotan_all = (
-        lax.all_gather(inputs, "col", axis=0, tiled=True),
+        jnp.concatenate(
+            lax.all_to_all(jnp.stack([inputs] * lax.axis_size("col")), "col", 0, 0), axis=0
+        ),
         lax.all_gather(cotangent, "col", axis=0, tiled=True),
     )
     grad_hidden = lax.psum_scatter(

time: 341 us -> 340 us (level)
  waiting for transfers between devices: 222 us -> 134 us
  blocking collectives: 0 us -> 87.7 us
    all_to_all x0 -> x1, blocking collectives: none -> 87.7 us  [per_device(): lax.all_to_all(jnp.stack([inputs] * lax.axis_size('col')), 'col', 0, 0)]
    reduce_scatter x1, waiting for transfers between devices: 48.4 us -> 0.01 us  [per_device(): lax.psum_scatter(contract_last(gate_grad_all, w_gate) + contract_last(up_...]
    all_gather x1 -> x0, waiting for transfers between devices: 39.4 us -> none  [per_device(): lax.all_gather(inputs, 'col', axis=0, tiled=True)]
  transfers between devices with their start and end apart: 7 -> 6, of which waited for: 6 -> 4; matrix products, arithmetic and copies ran while one was open for 26% -> 26% of each run, Pallas kernels for 0% -> 0%
where the time goes in v1:
time: 340 us
  waiting for transfers between devices  134 us (39%)
  blocking collectives  87.7 us (26%)
  matrix products  61.6 us (18%)
  local copies, waits for them, and re-layouts  36.6 us (11%)
  between operations  14.1 us (4%)
  other arithmetic  4.72 us (1%)
    all_to_all x1, blocking collectives, per_device(): lax.all_to_all(jnp.stack([inputs] * lax.axis_size('col')), 'col', 0, 0)  87.7 us
    all_gather x1, waiting for transfers between devices, per_device(): lax.all_gather(cotangent, 'col', axis=0, tiled=True)  54 us
    reduce_scatter x1, waiting for transfers between devices, per_device(): lax.psum_scatter(contract_last(cotan_all, w_down), 'row', scatter_dimensi...  43.2 us
    unnamed x12, local copies, waits for them, and re-layouts  36.4 us
    dot_general x3, matrix products, contract_last(): lax.dot_general(left, right, (((1,), (1,)), ((), ())), preferred_element_...  32.8 us
    dot_general x3, matrix products, contract_first(): lax.dot_general(left, right, (((0,), (0,)), ((), ())), preferred_element_...  28.8 us
    all_gather x1, waiting for transfers between devices, per_device(): lax.all_gather(grad_gate_pre, 'row', axis=0, tiled=True)  21.3 us
    all_gather x1, waiting for transfers between devices, per_device(): lax.all_gather(grad_up_pre, 'row', axis=0, tiled=True)  14 us
  transfers between devices with their start and end apart: 6, of which 4 were waited for; matrix products, arithmetic and copies ran while one was open for 26% of the time, Pallas kernels for 0%

profile of v1, /device:TPU:0, one launch (start us, length us, event | category | flops | bytes accessed | tf_op | source)
XLA Modules:
  0.0 339.6 jit_solution(10721222945920521104)
XLA Ops:
  7.2 0.0 all-gather.5.cloned.1.call-start
  7.2 0.7 all-gather.5.cloned.1.call-update
  7.9 0.0 reduce-scatter.3.cloned.1.call-start
  7.9 54.0 %all-gather.5.cloned.1.call-done = bf16[512,2048]{1,0:T(8,128)(2,1)} async-done(((bf16[64,2048]{1,0:T(8,128)(2,1)}), bf16[512,2048]{1,0:T(8,128)(2,1)}) %all-gather.5.cloned.1.call-update) | async-done | bytes 2097168 | tf_op jit(solution)/shard_map/all_gather | solution.py:36
  61.9 10.6 %fusion.8 = f32[512,2048]{1,0:T(8,128)} fusion(bf16[512,2048]{1,0:T(8,128)(2,1)} %all-gather.5.cloned.1.call-done, bf16[2048,2048]{1,0:T(8,128)(2,1)} %param.13), kind=kOutput, calls=%fused_computation.18 | convolution fusion | flops 4294967296 | bytes 14680064 | tf_op jit(solution)/shard_map/dot_general | solution.py:20
  72.5 0.0 reduce-scatter.3.cloned.1.call-update
  72.5 0.0 all-gather.7.cloned.1.call-start
  72.6 43.2 %reduce-scatter.3.cloned.1.call-done = f32[128,2048]{1,0:T(8,128)} async-done(((f32[512,2048]{1,0:T(8,128)}), f32[128,2048]{1,0:T(8,128)}) %reduce-scatter.3.cloned.1.call-update) | async-done | bytes 1048592 | tf_op jit(solution)/shard_map/reduce_scatter | solution.py:38
  115.8 0.0 copy-done
  115.8 0.0 copy-done.1
  115.8 2.9 multiply_convert_fusion
  118.8 0.0 all-gather.7.cloned.1.call-update
  118.8 0.0 all-gather.9.cloned.1.call-start
  118.8 0.5 all-gather.9.cloned.1.call-update
  119.4 0.0 all-gather.11.cloned.1.call-start
  119.4 0.5 all-gather.11.cloned.1.call-update
  119.9 0.2 reduce-scatter.5.cloned.1.call-start
  120.2 21.3 %all-gather.7.cloned.1.call-done = bf16[512,2048]{1,0:T(8,128)(2,1)} async-done(((bf16[128,2048]{1,0:T(8,128)(2,1)}), bf16[512,2048]{1,0:T(8,128)(2,1)}) %all-gather.7.cloned.1.call-update) | async-done | bytes 2097168 | tf_op jit(solution)/shard_map/all_gather | solution.py:44
  141.5 10.6 %fusion.9 = f32[512,2048]{1,0:T(8,128)} fusion(bf16[512,2048]{1,0:T(8,128)(2,1)} %all-gather.7.cloned.1.call-done, bf16[2048,2048]{1,0:T(8,128)(2,1)} %param.11), kind=kOutput, calls=%fused_computation.19 | convolution fusion | flops 4294967296 | bytes 14680064 | tf_op jit(solution)/shard_map/dot_general | solution.py:20
  152.1 14.0 %all-gather.9.cloned.1.call-done = bf16[512,2048]{1,0:T(8,128)(2,1)} async-done(((bf16[128,2048]{1,0:T(8,128)(2,1)}), bf16[512,2048]{1,0:T(8,128)(2,1)}) %all-gather.9.cloned.1.call-update) | async-done | bytes 2097168 | tf_op jit(solution)/shard_map/all_gather | solution.py:45
  166.1 11.7 %convolution_add_fusion = f32[512,2048]{1,0:T(8,128)} fusion(f32[512,2048]{1,0:T(8,128)} %fusion.9, bf16[512,2048]{1,0:T(8,128)(2,1)} %all-gather.9.cloned.1.call-done, bf16[2048,2048]{1,0:T(8,128)(2,1)} %param.12), kind=kOutput, calls=%fused_computation.3 | convolution fusion | flops 4296015872 | bytes 18874368 | tf_op jit(solution)/shard_map/dot_general | solution.py:20
  177.7 0.0 reduce-scatter.5.cloned.1.call-update
  177.8 0.9 copy-done.2
  178.7 0.2 stack.2
  178.9 87.7 %all_to_all.5 = bf16[8,64,2048]{2,1,0:T(8,128)(2,1)S(1)} all-to-all(bf16[8,64,2048]{2,1,0:T(8,128)(2,1)S(1)} %stack.2), channel_id=1, replica_groups=mesh['row'=4,'col'=8] {'col'}, dimensions={0} | all-to-all | bytes 4194304 | tf_op jit(solution)/shard_map/all_to_all | solution.py:34
  266.7 0.0 copy-done.4
  266.7 8.6 %multiply_bitcast_fusion.1 = f32[2048,2048]{0,1:T(8,128)} fusion(bf16[512,2048]{1,0:T(8,128)(2,1)S(1)} %copy-done.4, bf16[512,2048]{1,0:T(8,128)(2,1)S(1)} %bitcast.17), kind=kOutput, calls=%fused_computation.1 | convolution fusion | flops 4299161600 | bytes 20971520 | tf_op jit(solution)/shard_map/dot_general | solution.py:26
  275.3 17.7 %copy.11 = f32[2048,2048]{1,0:T(8,128)} copy(f32[2048,2048]{0,1:T(8,128)} %multiply_bitcast_fusion.1) | data formatting | bytes 33554432
  292.9 10.1 %multiply_bitcast_fusion = f32[2048,2048]{0,1:T(8,128)} fusion(bf16[512,2048]{1,0:T(8,128)(2,1)} %all-gather.9.cloned.1.call-done, bf16[512,2048]{1,0:T(8,128)(2,1)S(1)} %bitcast.18), kind=kOutput, calls=%fused_computation | convolution fusion | flops 4299161600 | bytes 20971520 | tf_op jit(solution)/shard_map/dot_general | solution.py:26
  303.1 17.8 %copy.12 = f32[2048,2048]{1,0:T(8,128)} copy(f32[2048,2048]{0,1:T(8,128)} %multiply_bitcast_fusion) | data formatting | bytes 33554432
  320.8 10.1 %convolution_multiply_fusion = f32[2048,2048]{1,0:T(8,128)} fusion(bf16[512,2048]{1,0:T(8,128)(2,1)} %all-gather.11.cloned.1.call-done, bf16[512,2048]{1,0:T(8,128)(2,1)S(1)} %copy-done.3), kind=kOutput, calls=%fused_computation.2 | convolution fusion | flops 4299161600 | bytes 20971520 | tf_op jit(solution)/shard_map/dot_general | solution.py:26
  331.0 1.8 convert_element_type.22
  (8 shorter events, 0.0 us)
Async XLA Ops:
  7.2 54.8 %all-gather.5.cloned.1.call-start = ((), (), s32[]{:S(2)}) async-start(), calls=%async_computation.3 | async-start | bytes 2359296 | tf_op jit(solution)/shard_map/all_gather | solution.py:36
  7.9 107.9 %reduce-scatter.3.cloned.1.call-start = ((), (), s32[]{:S(2)}) async-start(), calls=%async_computation.4 | async-start | bytes 5242880 | tf_op jit(solution)/shard_map/reduce_scatter | solution.py:38
  72.5 43.3 %copy-start = (bf16[128,2048]{1,0:T(8,128)(2,1)S(1)}, bf16[128,2048]{1,0:T(8,128)(2,1)}, u32[]{:S(2)}) copy-start(bf16[128,2048]{1,0:T(8,128)(2,1)} %param.9) | copy-start | bytes 1572868
  72.5 43.3 %copy-start.1 = (bf16[128,2048]{1,0:T(8,128)(2,1)S(1)}, bf16[128,2048]{1,0:T(8,128)(2,1)}, u32[]{:S(2)}) copy-start(bf16[128,2048]{1,0:T(8,128)(2,1)} %param.10) | copy-start | bytes 1572868
  72.5 69.0 %all-gather.7.cloned.1.call-start = ((), (), s32[]{:S(2)}) async-start(), calls=%async_computation.5 | async-start | bytes 2621440 | tf_op jit(solution)/shard_map/all_gather | solution.py:44
  118.8 47.3 %all-gather.9.cloned.1.call-start = ((), (), s32[]{:S(2)}) async-start(), calls=%async_computation.6 | async-start | bytes 2621440 | tf_op jit(solution)/shard_map/all_gather | solution.py:45
  119.4 201.5 %all-gather.11.cloned.1.call-start = ((), (), s32[]{:S(2)}) async-start(), calls=%async_computation.8 | async-start | bytes 2621440 | tf_op jit(solution)/shard_map/all_gather | solution.py:43
  119.9 211.0 %reduce-scatter.5.cloned.1.call-start = ((), (), s32[]{:S(2)}) async-start(), calls=%async_computation.7 | async-start | bytes 4718592 | tf_op jit(solution)/shard_map/reduce_scatter | solution.py:47
  177.7 0.9 copy-start.2
  178.7 88.0 %copy-start.4 = (bf16[512,2048]{1,0:T(8,128)(2,1)S(1)}, bf16[512,2048]{1,0:T(8,128)(2,1)}, u32[]{:S(2)}) copy-start(bf16[512,2048]{1,0:T(8,128)(2,1)} %all-gather.7.cloned.1.call-done) | copy-start | bytes 6291460
  303.0 17.8 %copy-start.3 = (bf16[512,2048]{1,0:T(8,128)(2,1)S(1)}, bf16[512,2048]{1,0:T(8,128)(2,1)}, u32[]{:S(2)}) copy-start(bf16[512,2048]{1,0:T(8,128)(2,1)} %all-gather.5.cloned.1.call-done) | copy-start | bytes 6291460
Sparse Core Ops, SparseCore 0:
  10.1 51.7 all-gather.4
  72.7 43.1 reduce-scatter.2
  118.9 22.5 all-gather.6
  143.5 22.5 all-gather.8
  167.5 22.5 all-gather.10
  193.6 116.0 reduce-scatter.4
